TPU v7x, 256 devices: a whole 4x4x8 slice. The times are simulated.
256 devices in a mesh: cache: 32 (over x, z), owner: 8 (over y, core).
Axes of the slice: x: 4, y: 4, z: 8, core: 2. Of those that a mesh axis runs over, the one named last changes fastest.
Arguments:
- cache: bfloat16 [32, 4, 128, 256], P('cache'), may hold values from -2.5 to 2.5
- backing: bfloat16 [32, 64, 128, 256], P('cache', 'owner'), may hold values from -2.5 to 2.5
- resident: int32 [32, 4], P('cache'), may hold values from 0 to 63, as said below
- promote: int32 [32, 2], P('cache'), may hold values from 0 to 63, as said below
- victim: int32 [32, 2], P('cache'), may hold values from 0 to 3, as said below
- lookups: int32 [2, 32768, 32, 8], P(None, 'owner', 'cache'), may hold values from 0 to 511
- route: int32 [2, 8, 4096], P(None, 'owner'), may hold values from 0 to 4095, each once within a row
- dcn_down: bfloat16 [8192, 128], P('cache'), may hold values from -0.0625 to 0.0625
- dcn_up: bfloat16 [128, 8192], P(None, 'cache'), may hold values from -0.5 to 0.5
- dcn_bias: float32 [8192], replicated, may hold values from -5 to 5
- mlp_in: bfloat16 [8192, 1024], P('cache'), may hold values from -0.0625 to 0.0625
- mlp_bias: float32 [1024], replicated, may hold values from -3 to 3
- mlp_out: float32 [1024], replicated, may hold values from -0.1875 to 0.1875
- out_bias: float32 [1], replicated, may hold values from -4 to 4
Outputs:
- scores: float32 [2, 8, 4096], P(None, 'owner', 'cache')
- new_cache: bfloat16 [32, 4, 128, 256], P('cache')
- new_backing: bfloat16 [32, 64, 128, 256], P('cache', 'owner')
Inputs may be any that keep to these rules, and one draw needn't show every extreme that they name: `resident`: for each feature, 4 distinct backing blocks. `promote`: for each feature, 2 distinct backing blocks, none of them in that feature's resident; block k belongs to owner k // 8. `victim`: for each feature, 2 distinct slots. `route`: each batch and owner group holds every request index once.
All inputs are finite; a program needn't handle non-finite values.
Results may differ from a plain program's by a relative error of at most 0.004.
Values may be sent and summed in bfloat16 or wider, within the bound.
No kernel may reach another device: no remote copies, remote signals or barrier semaphores. Data moves between devices by JAX's collectives and lax.ppermute only.
A program may use at most 128 MiB of HBM per device.

v0:
```python
import jax
import jax.numpy as jnp
from jax import lax
from jax.sharding import PartitionSpec as P


def copy_for_each(x, axis):
    size = lax.axis_size(axis)
    return lax.all_to_all(jnp.broadcast_to(x[None], (size, *x.shape)), axis, 0, 0, tiled=True)


def in_order(blocks, dim):
    lengths = list(blocks.shape[1:])
    lengths[dim] *= blocks.shape[0]
    return jnp.moveaxis(blocks, 0, dim).reshape(lengths)


def gathered_copies(x, axis, dim):
    blocks = copy_for_each(x, axis)
    return in_order(blocks, dim)


def take_rows(table, wanted):
    return jax.vmap(lambda rows, chosen: rows[chosen])(table, wanted)


def pool_batch(requests, order, table):
    requests = requests[order]
    count = requests.shape[0]
    step = min(512, count)
    codes = jnp.arange(table.shape[1], dtype=jnp.int32)

    def one_block(lookup_block):
        counts = jnp.sum((lookup_block[..., None] == codes).astype(jnp.bfloat16), axis=2)
        return jnp.einsum("rfk,fke->rfe", counts, table, preferred_element_type=jnp.float32).astype(
            jnp.bfloat16
        )

    blocks = requests.reshape((count // step, step) + requests.shape[1:])
    pooled = lax.map(one_block, blocks)
    return pooled.reshape((count,) + pooled.shape[2:])


def on_device(
    cache,
    backing,
    resident,
    promote,
    victim,
    lookups,
    route,
    dcn_down,
    dcn_up,
    dcn_bias,
    mlp_in,
    mlp_bias,
    mlp_out,
    out_bias,
):
    held = cache.shape[0]
    slots = cache.shape[1]
    block = cache.shape[2]
    width = cache.shape[3]
    own_blocks = backing.shape[1]
    promoted_count = promote.shape[1]
    owner_here = lax.axis_index("owner")
    local_index = promote - owner_here * own_blocks
    owned_here = (local_index >= 0) & (local_index < own_blocks)
    clamped = jnp.clip(local_index, 0, own_blocks - 1)
    fetched = take_rows(backing, clamped)
    outgoing = jnp.where(owned_here[:, :, None, None], fetched, jnp.zeros_like(fetched))
    arrived = gathered_copies(outgoing, "owner", 0)
    owners = arrived.shape[0] // held
    arrived = arrived.reshape(owners, held, promoted_count, block, width)
    source = promote // own_blocks
    picked = source[None] == jnp.arange(owners, dtype=jnp.int32)[:, None, None]
    promoted = jnp.sum(jnp.where(picked[..., None, None], arrived, jnp.zeros_like(arrived)), axis=0)
    evicted = take_rows(cache, victim)
    leaving = take_rows(resident, victim) - owner_here * own_blocks
    slot_numbers = jnp.arange(slots, dtype=jnp.int32)
    block_numbers = jnp.arange(own_blocks, dtype=jnp.int32)
    new_cache = cache
    new_backing = backing
    for column in range(promoted_count):
        slot_hit = victim[:, column][:, None] == slot_numbers[None, :]
        new_cache = jnp.where(slot_hit[:, :, None, None], promoted[:, column][:, None], new_cache)
        block_hit = leaving[:, column][:, None] == block_numbers[None, :]
        new_backing = jnp.where(
            block_hit[:, :, None, None], evicted[:, column][:, None], new_backing
        )
    table = new_cache.reshape(held, slots * block, width)
    batches = lookups.shape[0]
    received = []
    for batch_turn in range(batches):
        pooled = pool_batch(lookups[batch_turn], route[batch_turn, 0], table)
        received.append(lax.all_to_all(pooled, "cache", split_axis=0, concat_axis=1, tiled=True))
    arrived_rows = jnp.stack(received)
    per_batch = arrived_rows.shape[1]
    features = arrived_rows.reshape(batches * per_batch, -1)
    columns = features
    low = jnp.dot(
        columns,
        lax.all_gather(dcn_down, "cache", axis=0, tiled=True),
        preferred_element_type=jnp.float32,
    ).astype(jnp.bfloat16)
    gate = (
        jnp.dot(
            low,
            lax.all_gather(dcn_up, "cache", axis=1, tiled=True),
            preferred_element_type=jnp.float32,
        )
        + dcn_bias
    )
    crossed = (features * gate + features).astype(jnp.bfloat16)
    columns = crossed
    before = jnp.dot(
        columns,
        lax.all_gather(mlp_in, "cache", axis=0, tiled=True),
        preferred_element_type=jnp.float32,
    )
    hidden = jnp.maximum(before + mlp_bias, 0.0)
    scores = jnp.sum(hidden * mlp_out, axis=-1) + out_bias[0]
    return (scores.reshape(batches, 1, per_batch), new_cache, new_backing)


def solution(mesh):
    in_specs = (
        P("cache", None, None, None),
        P("cache", "owner", None, None),
        P("cache", None),
        P("cache", None),
        P("cache", None),
        P(None, "owner", "cache", None),
        P(None, "owner", None),
        P("cache", None),
        P(None, "cache"),
        P(),
        P("cache", None),
        P(),
        P(),
        P(),
    )
    out_specs = (
        P(None, "owner", "cache"),
        P("cache", None, None, None),
        P("cache", "owner", None, None),
    )
    return jax.shard_map(
        on_device, mesh=mesh, in_specs=in_specs, out_specs=out_specs, check_vma=False
    )
```

profile of v0, /device:TPU:1, one launch (start us, length us, event | category | flops | bytes accessed | tf_op | source)
XLA Modules:
  0.0 363.3 jit_solution(7484960167387886002)
XLA Ops:
  13.9 6.7 %all-to-all-start = ((bf16[8,1,2,128,256]{4,3,2,1,0:T(8,128)(2,1)}), bf16[8,1,2,128,256]{4,3,2,1,0:T(8,128)(2,1)S(1)}, u32[]{:S(2)}, u32[]{:S(2)}) async-start(bf16[8,1,2,128,256]{4,3,2,1,0:T(8,128)(2,1)} %broadcast_in_dim.137), calls=%async_computation | async-start | bytes 2097152 | tf_op jit(solution)/shard_map/all_to_all | solution.py:9
  21.2 14.1 %gather_fusion = s32[4096,8]{1,0:T(8,128)} fusion(s32[4096,8]{1,0:T(8,128)S(1)} %bitcast.111, s32[4096]{0:T(1024)S(1)} %broadcast_clamp_fusion.1), kind=kCustom, calls=%fused_computation | custom fusion | bytes 278528 | tf_op jit(solution)/shard_map/gather | solution.py:28
  38.8 14.1 %gather_fusion.1 = s32[4096,8]{1,0:T(8,128)} fusion(s32[4096,8]{1,0:T(8,128)S(1)} %bitcast.110, s32[4096]{0:T(1024)S(1)} %broadcast_clamp_fusion), kind=kCustom, calls=%fused_computation.1 | custom fusion | bytes 278528 | tf_op jit(solution)/shard_map/gather | solution.py:28
  57.6 35.3 %while.26 = (s32[]{:T(128)}, bf16[8,512,1,256]{3,1,2,0:T(8,128)(2,1)S(1)}, s32[8,512,1,8]{1,3,2,0:T(8,128)}, bf16[1,512,256]{2,1,0:T(8,128)(2,1)S(1)}, s32[]{:T(128)}) while((s32[]{:T(128)}, bf16[8,512,1,256]{3,1,2,0:T(8,128)(2,1)S(1)}, s32[8,512,1,8]{1,3,2,0:T(8,128)}, bf16[1,512,256]{2,1,0:T(8,128)(2,1)S(1)}, s32[]{:T(128)}) %tuple.90), condition=%wide.region_3.4_spmd.clone, body=%wide.region_1.3_spmd.clone.sunk | while | flops 140378112 | bytes 1654853 | solution.py:40
  58.4 3.2 fusion.41
  62.8 3.2 fusion.41
  67.2 3.2 fusion.41
  76.1 3.2 fusion.41
  80.5 3.2 fusion.41
  84.9 3.2 fusion.41
  89.3 3.2 fusion.41
  96.3 4.0 %reshape.321 = bf16[32,2,16384]{2,1,0:T(2,128)(2,1)} reshape(bf16[4096,256]{1,0:T(8,128)(2,1)} %reduce.17) | data formatting | bytes 4194304
  100.3 10.3 %all-to-all-start.1 = ((bf16[32,2,16384]{2,1,0:T(2,128)(2,1)}), bf16[32,2,16384]{2,1,0:T(2,128)(2,1)S(1)}, u32[]{:S(2)}, u32[]{:S(2)}) async-start(bf16[32,2,16384]{2,1,0:T(2,128)(2,1)} %reshape.321), calls=%async_computation.1 | async-start | bytes 4194304 | tf_op jit(solution)/shard_map/all_to_all | solution.py:96
  112.1 35.1 %while.27 = (s32[]{:T(128)}, bf16[8,512,1,256]{3,1,2,0:T(8,128)(2,1)}, s32[8,512,1,8]{1,3,2,0:T(8,128)S(1)}, bf16[1,512,256]{2,1,0:T(8,128)(2,1)S(1)}, s32[]{:T(128)}) while((s32[]{:T(128)}, bf16[8,512,1,256]{3,1,2,0:T(8,128)(2,1)}, s32[8,512,1,8]{1,3,2,0:T(8,128)S(1)}, bf16[1,512,256]{2,1,0:T(8,128)(2,1)S(1)}, s32[]{:T(128)}) %tuple.91), condition=%wide.region_6.7_spmd.clone, body=%wide.region_4.6_spmd.clone.sunk | while | flops 140378112 | bytes 1655361 | solution.py:40
  112.2 3.2 fusion.45
  116.6 3.2 fusion.45
  121.0 3.2 fusion.45
  125.4 3.2 fusion.45
  129.8 3.2 fusion.45
  134.2 3.2 fusion.45
  138.6 3.2 fusion.45
  147.2 4.5 %reduce.16 = bf16[4096,256]{1,0:T(8,128)(2,1)} reduce(bf16[4096,1,256]{2,0,1:T(8,128)(2,1)} %bitcast.116, bf16[]{:T(256)} %broadcast.259), dimensions={1}, to_apply=%copy.68.reduce_sub_computation | reduce | bytes 4194306 | tf_op jit(solution)/shard_map/reshape | solution.py:41
  151.7 4.0 %reshape.319 = bf16[32,2,16384]{2,1,0:T(2,128)(2,1)} reshape(bf16[4096,256]{1,0:T(8,128)(2,1)} %reduce.16) | data formatting | bytes 4194304
  155.7 6.3 %all-to-all-done.1 = bf16[32,2,16384]{2,1,0:T(2,128)(2,1)S(1)} async-done(((bf16[32,2,16384]{2,1,0:T(2,128)(2,1)}), bf16[32,2,16384]{2,1,0:T(2,128)(2,1)S(1)}, u32[]{:S(2)}, u32[]{:S(2)}) %all-to-all-start.1) | async-done | bytes 2097184 | tf_op jit(solution)/shard_map/all_to_all | solution.py:96
  162.0 10.4 %all-to-all-start.2 = ((bf16[32,2,16384]{2,1,0:T(2,128)(2,1)}), bf16[32,2,16384]{2,1,0:T(2,128)(2,1)}, u32[]{:S(2)}, u32[]{:S(2)}) async-start(bf16[32,2,16384]{2,1,0:T(2,128)(2,1)} %reshape.319), calls=%async_computation.2 | async-start | bytes 4194304 | tf_op jit(solution)/shard_map/all_to_all | solution.py:96
  177.5 6.7 %reshape.322 = bf16[4096,1,256]{2,1,0:T(2,128)(2,1)} reshape(bf16[32,2,16384]{2,1,0:T(2,128)(2,1)S(1)} %all-to-all-done.1) | data formatting | bytes 4194304
  186.8 41.1 %all-to-all-done.2 = bf16[32,2,16384]{2,1,0:T(2,128)(2,1)} async-done(((bf16[32,2,16384]{2,1,0:T(2,128)(2,1)}), bf16[32,2,16384]{2,1,0:T(2,128)(2,1)}, u32[]{:S(2)}, u32[]{:S(2)}) %all-to-all-start.2) | async-done | bytes 2097184 | tf_op jit(solution)/shard_map/all_to_all | solution.py:96
  227.9 10.4 %reshape.320 = bf16[4096,1,256]{2,1,0:T(2,128)(2,1)} reshape(bf16[32,2,16384]{2,1,0:T(2,128)(2,1)} %all-to-all-done.2) | data formatting | bytes 4194304
  243.7 6.2 %copy.77 = bf16[32,8,32,256]{3,1,2,0:T(8,128)(2,1)} copy(bf16[32,8,32,256]{3,2,1,0:T(8,128)(2,1)S(1)} %bitcast.114) | data formatting | bytes 8388608
  249.9 4.1 %convolution_convert_fusion.2 = bf16[256,128]{1,0:T(8,128)(2,1)S(1)} fusion(bf16[256,8192]{1,0:T(8,128)(2,1)} %bitcast.112, bf16[8192,128]{1,0:T(8,128)(2,1)} %all-gather.4.cloned.1.call-done), kind=kOutput, calls=%fused_computation.31 | convolution fusion | flops 536903680 | bytes 6356992 | tf_op jit(solution)/shard_map/dot_general | solution.py:101
  254.1 89.4 %all-gather.8.cloned.1.call-done = bf16[8192,1024]{1,0:T(8,128)(2,1)} async-done(((bf16[256,1024]{1,0:T(8,128)(2,1)}), bf16[8192,1024]{1,0:T(8,128)(2,1)}) %all-gather.8.cloned.1.call-update) | async-done | bytes 16777232 | tf_op jit(solution)/shard_map/all_gather | solution.py:118
  343.5 12.7 %fusion.17 = f32[256]{0:T(256)S(1)} fusion(bf16[8192,1024]{1,0:T(8,128)(2,1)} %all-gather.8.cloned.1.call-done, bf16[256,128]{1,0:T(8,128)(2,1)S(1)} %convolution_convert_fusion.2, bf16[128,8192]{1,0:T(8,128)(2,1)} %all-gather.6.cloned.1.call-done, bf16[256,8192]{1,0:T(8,128)(2,1)} %bitcast.113, f32[8192]{0:T(1024)S(1)} %copy-done.8, ...), kind=kOutput, calls=%fused_computation.30 | convolution fusion | flops 4843372544 | bytes 23176192 | tf_op jit(solution)/shard_map/dot_general | solution.py:116
  (123 shorter events, 58.0 us)
Async XLA Ops:
  7.2 166.8 %copy-start = (s32[1,4]{1,0:T(1,128)S(1)}, s32[1,4]{1,0:T(1,128)}, u32[]{:S(2)}) copy-start(s32[1,4]{1,0:T(1,128)} %param.20) | copy-start | bytes 52
  7.2 242.7 %all-gather.4.cloned.1.call-start = ((), (), s32[]{:S(2)}) async-start(), calls=%async_computation.3 | async-start | bytes 2162688 | tf_op jit(solution)/shard_map/all_gather | solution.py:103
  7.9 246.2 %all-gather.6.cloned.1.call-start = ((), (), s32[]{:S(2)}) async-start(), calls=%async_computation.4 | async-start | bytes 2162688 | tf_op jit(solution)/shard_map/all_gather | solution.py:109
  8.7 11.9 %copy-start.5 = (s32[2,4096,1,8]{1,3,2,0:T(8,128)S(1)}, s32[2,4096,1,8]{1,3,2,0:T(8,128)}, u32[]{:S(2)}) copy-start(s32[2,4096,1,8]{1,3,2,0:T(8,128)} %param.23) | copy-start | bytes 786436
  8.7 334.8 %all-gather.8.cloned.1.call-start = ((), (), s32[]{:S(2)}) async-start(), calls=%async_computation.5 | async-start | bytes 17301504 | tf_op jit(solution)/shard_map/all_gather | solution.py:118
  12.0 8.5 %copy-start.6 = (s32[2,1,4096]{2,1,0:T(1,128)S(1)}, s32[2,1,4096]{2,1,0:T(1,128)}, u32[]{:S(2)}) copy-start(s32[2,1,4096]{2,1,0:T(1,128)} %param.24) | copy-start | bytes 98308
  13.9 43.2 %all-to-all-start = ((bf16[8,1,2,128,256]{4,3,2,1,0:T(8,128)(2,1)}), bf16[8,1,2,128,256]{4,3,2,1,0:T(8,128)(2,1)S(1)}, u32[]{:S(2)}, u32[]{:S(2)}) async-start(bf16[8,1,2,128,256]{4,3,2,1,0:T(8,128)(2,1)} %broadcast_in_dim.137), calls=%async_computation | async-start | bytes 2097152 | tf_op jit(solution)/shard_map/all_to_all | solution.py:9
  52.9 2.2 copy-start.7
  52.9 4.4 %copy-start.3 = (bf16[1,4,128,256]{3,2,1,0:T(8,128)(2,1)S(1)}, bf16[1,4,128,256]{3,2,1,0:T(8,128)(2,1)}, u32[]{:S(2)}) copy-start(bf16[1,4,128,256]{3,2,1,0:T(8,128)(2,1)} %param.18) | copy-start | bytes 786436
  100.3 61.7 %all-to-all-start.1 = ((bf16[32,2,16384]{2,1,0:T(2,128)(2,1)}), bf16[32,2,16384]{2,1,0:T(2,128)(2,1)S(1)}, u32[]{:S(2)}, u32[]{:S(2)}) async-start(bf16[32,2,16384]{2,1,0:T(2,128)(2,1)} %reshape.321), calls=%async_computation.1 | async-start | bytes 4194304 | tf_op jit(solution)/shard_map/all_to_all | solution.py:96
  147.2 4.5 %copy-start.4 = (bf16[1,512,256]{2,1,0:T(8,128)(2,1)}, bf16[1,512,256]{2,1,0:T(8,128)(2,1)S(1)}, u32[]{:S(2)}) copy-start(bf16[1,512,256]{2,1,0:T(8,128)(2,1)S(1)} %get-tuple-element.330) | copy-start | bytes 786436
  155.7 20.8 %copy-start.2 = (bf16[1,8,128,256]{3,2,1,0:T(8,128)(2,1)S(1)}, bf16[1,8,128,256]{3,2,1,0:T(8,128)(2,1)}, u32[]{:S(2)}) copy-start(bf16[1,8,128,256]{3,2,1,0:T(8,128)(2,1)} %param.19) | copy-start | bytes 1572868
  162.0 65.9 %all-to-all-start.2 = ((bf16[32,2,16384]{2,1,0:T(2,128)(2,1)}), bf16[32,2,16384]{2,1,0:T(2,128)(2,1)}, u32[]{:S(2)}, u32[]{:S(2)}) async-start(bf16[32,2,16384]{2,1,0:T(2,128)(2,1)} %reshape.319), calls=%async_computation.2 | async-start | bytes 4194304 | tf_op jit(solution)/shard_map/all_to_all | solution.py:96
  249.9 93.6 %copy-start.8 = (f32[8192]{0:T(1024)S(1)}, f32[8192]{0:T(1024)}, u32[]{:S(2)}) copy-start(f32[8192]{0:T(1024)} %param.27) | copy-start | bytes 98308
  249.9 93.6 %copy-start.9 = (f32[1024]{0:T(1024)S(1)}, f32[1024]{0:T(1024)}, u32[]{:S(2)}) copy-start(f32[1024]{0:T(1024)} %param.30) | copy-start | bytes 12292
  249.9 93.6 %copy-start.10 = (f32[1024]{0:T(1024)S(1)}, f32[1024]{0:T(1024)}, u32[]{:S(2)}) copy-start(f32[1024]{0:T(1024)} %param.29) | copy-start | bytes 12292
  343.5 13.2 %copy-start.1 = (s32[1,4]{1,0:T(1,128)S(1)}, s32[1,4]{1,0:T(1,128)}, u32[]{:S(2)}) copy-start(s32[1,4]{1,0:T(1,128)} %param.20) | copy-start | bytes 52
Sparse Core Ops, SparseCore 0:
  10.6 77.0 all-gather.3
  90.1 95.1 all-gather.5
  187.9 155.6 all-gather.7
where the time goes:
time: 365 us; the launch traced here: 363 us
  waiting for transfers between devices  139 us (38%)
  local copies, waits for them, and re-layouts  88.8 us (24%)
  other arithmetic  65.7 us (18%)
  starting transfers between devices  27.5 us (8%)
  matrix products  27.3 us (7%)
  between operations  14.7 us (4%)
    all_gather x1, waiting for transfers between devices, on_device(): lax.all_gather(mlp_in, 'cache', axis=0, tiled=True)  89.4 us
    reduce_sum x16, other arithmetic, one_block(): jnp.sum((lookup_block[..., None] == codes).astype(jnp.bfloat16), axis=2)  51.7 us
    all_to_all x2, waiting for transfers between devices, on_device(): lax.all_to_all(pooled, 'cache', split_axis=0, concat_axis=1, tiled=True)  47.4 us
    unnamed x35, local copies, waits for them, and re-layouts  42.9 us
    gather x2, local copies, waits for them, and re-layouts, pool_batch(): requests = requests[order]  28.2 us
    all_to_all x2, starting transfers between devices, on_device(): lax.all_to_all(pooled, 'cache', split_axis=0, concat_axis=1, tiled=True)  20.7 us
    dot_general x1, matrix products, on_device(): jnp.dot(columns, lax.all_gather(mlp_in, 'cache', axis=0, tiled=True), pre...  12.7 us
    dot_general x16, matrix products, one_block(): jnp.einsum('rfk,fke->rfe', counts, table, preferred_element_type=jnp.floa...  10.5 us
  transfers between devices with their start and end apart: 6, of which 3 were waited for; matrix products, arithmetic and copies ran while one was open for 46% of the time, Pallas kernels for 0%

commit v1 on v0

--- a/solution.py
+++ b/solution.py
@@ -2,6 +2,13 @@
 import jax.numpy as jnp
 from jax import lax
 from jax.sharding import PartitionSpec as P
+
+
+def trade_parts(block, name, split, join):
+    size = lax.axis_size(name)
+    pieces = jnp.stack(jnp.split(block, size, axis=split), axis=0)
+    pieces = lax.all_to_all(pieces, name, split_axis=0, concat_axis=0)
+    return jnp.concatenate(pieces, axis=join)
 
 
 def copy_for_each(x, axis):
@@ -93,7 +100,7 @@
     received = []
     for batch_turn in range(batches):
         pooled = pool_batch(lookups[batch_turn], route[batch_turn, 0], table)
-        received.append(lax.all_to_all(pooled, "cache", split_axis=0, concat_axis=1, tiled=True))
+        received.append(trade_parts(pooled, "cache", 0, 1))
     arrived_rows = jnp.stack(received)
     per_batch = arrived_rows.shape[1]
     features = arrived_rows.reshape(batches * per_batch, -1)

time: 365 us -> 373 us (1.022)
  waiting for transfers between devices: 139 us -> 153 us
  local copies, waits for them, and re-layouts: 88.8 us -> 96.5 us
  other arithmetic: 65.7 us -> 59.9 us
  matrix products: 27.3 us -> 21.6 us
    all_to_all x2, waiting for transfers between devices: 47.4 us -> 56.4 us  [trade_parts(): pieces = lax.all_to_all(pieces, name, split_axis=0, concat_axis=0)]
    unnamed x35 -> x89, local copies, waits for them, and re-layouts: 42.9 us -> 51.3 us
    reshape x2 -> x0, other arithmetic: 7.43 us -> none  [pool_batch(): return pooled.reshape((count,) + pooled.shape[2:])]
    dot_general x16, matrix products: 10.5 us -> 4.79 us  [one_block(): jnp.einsum('rfk,fke->rfe', counts, table, preferred_element_type=jnp.floa...]
    all_gather x1, waiting for transfers between devices: 89.4 us -> 94.1 us  [on_device(): lax.all_gather(mlp_in, 'cache', axis=0, tiled=True)]
  transfers between devices with their start and end apart: 6 -> 6, of which waited for: 3 -> 3; matrix products, arithmetic and copies ran while one was open for 46% -> 44% of each run, Pallas kernels for 0% -> 0%
where the time goes in v1:
time: 373 us; the launch traced here: 372 us
  waiting for transfers between devices  153 us (41%)
  local copies, waits for them, and re-layouts  96.5 us (26%)
  other arithmetic  59.9 us (16%)
  starting transfers between devices  26.2 us (7%)
  matrix products  21.6 us (6%)
  between operations  14.7 us (4%)
    all_gather x1, waiting for transfers between devices, on_device(): lax.all_gather(mlp_in, 'cache', axis=0, tiled=True)  94.1 us
    all_to_all x2, waiting for transfers between devices, trade_parts(): pieces = lax.all_to_all(pieces, name, split_axis=0, concat_axis=0)  56.4 us
    reduce_sum x16, other arithmetic, one_block(): jnp.sum((lookup_block[..., None] == codes).astype(jnp.bfloat16), axis=2)  51.7 us
    unnamed x89, local copies, waits for them, and re-layouts  51.3 us
    gather x2, local copies, waits for them, and re-layouts, pool_batch(): requests = requests[order]  28.2 us
    all_to_all x2, starting transfers between devices, trade_parts(): pieces = lax.all_to_all(pieces, name, split_axis=0, concat_axis=0)  19.5 us
    dot_general x1, matrix products, on_device(): jnp.dot(columns, lax.all_gather(mlp_in, 'cache', axis=0, tiled=True), pre...  12.7 us
    eq x32, local copies, waits for them, and re-layouts, one_block(): lookup_block[..., None] == codes  7.82 us
  transfers between devices with their start and end apart: 6, of which 3 were waited for; matrix products, arithmetic and copies ran while one was open for 44% of the time, Pallas kernels for 0%

profile of v1, /device:TPU:1, one launch (start us, length us, event | category | flops | bytes accessed | tf_op | source)
XLA Modules:
  0.0 372.1 jit_solution(443925231839151901)
XLA Ops:
  13.9 6.7 %all-to-all-start = ((bf16[8,1,2,128,256]{4,3,2,1,0:T(8,128)(2,1)}), bf16[8,1,2,128,256]{4,3,2,1,0:T(8,128)(2,1)S(1)}, u32[]{:S(2)}, u32[]{:S(2)}) async-start(bf16[8,1,2,128,256]{4,3,2,1,0:T(8,128)(2,1)} %broadcast_in_dim.137), calls=%async_computation | async-start | bytes 2097152 | tf_op jit(solution)/shard_map/all_to_all | solution.py:16
  21.2 14.1 %gather_fusion = s32[4096,8]{1,0:T(8,128)} fusion(s32[4096,8]{1,0:T(8,128)S(1)} %bitcast.364, s32[4096]{0:T(1024)S(1)} %get-tuple-element.226), kind=kCustom, calls=%fused_computation | custom fusion | bytes 278528 | tf_op jit(solution)/shard_map/gather | solution.py:35
  35.3 2.8 copy.178
  38.8 14.1 %gather_fusion.1 = s32[4096,8]{1,0:T(8,128)} fusion(s32[4096,8]{1,0:T(8,128)S(1)} %bitcast.365, s32[4096]{0:T(1024)S(1)} %get-tuple-element.225), kind=kCustom, calls=%fused_computation.1 | custom fusion | bytes 278528 | tf_op jit(solution)/shard_map/gather | solution.py:35
  52.8 2.2 copy.180
  57.5 35.3 %while.26 = (s32[]{:T(128)}, bf16[8,512,1,256]{3,1,2,0:T(8,128)(2,1)S(1)}, s32[8,512,1,8]{1,3,2,0:T(8,128)}, bf16[1,512,256]{2,1,0:T(8,128)(2,1)S(1)}, s32[]{:T(128)}) while((s32[]{:T(128)}, bf16[8,512,1,256]{3,1,2,0:T(8,128)(2,1)S(1)}, s32[8,512,1,8]{1,3,2,0:T(8,128)}, bf16[1,512,256]{2,1,0:T(8,128)(2,1)S(1)}, s32[]{:T(128)}) %tuple.89), condition=%wide.region_3.4_spmd.clone, body=%wide.region_1.3_spmd.clone.sunk | while | flops 140378112 | bytes 1654853 | solution.py:47
  58.4 3.2 fusion.41
  62.8 3.2 fusion.41
  67.2 3.2 fusion.41
  71.6 3.2 fusion.41
  76.0 3.2 fusion.41
  80.4 3.2 fusion.41
  84.8 3.2 fusion.41
  89.2 3.2 fusion.41
  112.7 10.5 %all-to-all-start.1 = ((bf16[32,128,1,256]{3,1,2,0:T(8,128)(2,1)}), bf16[32,128,1,256]{3,1,2,0:T(8,128)(2,1)}, u32[]{:S(2)}, u32[]{:S(2)}) async-start(bf16[32,128,1,256]{3,1,2,0:T(8,128)(2,1)} %constant_dynamic-update-slice_fusion), calls=%async_computation.1 | async-start | bytes 4194304 | tf_op jit(solution)/shard_map/all_to_all | solution.py:10
  123.3 29.6 %while.27 = (s32[]{:T(128)}, bf16[8,512,1,256]{3,1,2,0:T(8,128)(2,1)S(1)}, s32[8,512,1,8]{1,3,2,0:T(8,128)S(1)}, bf16[1,512,256]{2,1,0:T(8,128)(2,1)S(1)}, s32[]{:T(128)}) while((s32[]{:T(128)}, bf16[8,512,1,256]{3,1,2,0:T(8,128)(2,1)S(1)}, s32[8,512,1,8]{1,3,2,0:T(8,128)S(1)}, bf16[1,512,256]{2,1,0:T(8,128)(2,1)S(1)}, ...), condition=%wide.region_6.7_spmd.clone, body=%wide.region_4.6_spmd.clone.sunk | while | flops 140378112 | bytes 1654853 | solution.py:47
  123.5 3.2 fusion.45
  127.2 3.2 fusion.45
  130.9 3.2 fusion.45
  134.6 3.2 fusion.45
  138.3 3.2 fusion.45
  142.0 3.2 fusion.45
  145.7 3.2 fusion.45
  149.4 3.2 fusion.45
  172.9 4.3 %all-to-all-done.1 = bf16[32,128,1,256]{3,1,2,0:T(8,128)(2,1)} async-done(((bf16[32,128,1,256]{3,1,2,0:T(8,128)(2,1)}), bf16[32,128,1,256]{3,1,2,0:T(8,128)(2,1)}, u32[]{:S(2)}, u32[]{:S(2)}) %all-to-all-start.1) | async-done | bytes 2097184 | tf_op jit(solution)/shard_map/all_to_all | solution.py:10
  177.2 9.0 %all-to-all-start.2 = ((bf16[32,128,1,256]{3,1,2,0:T(8,128)(2,1)}), bf16[32,128,1,256]{3,1,2,0:T(8,128)(2,1)S(1)}, u32[]{:S(2)}, u32[]{:S(2)}) async-start(bf16[32,128,1,256]{3,1,2,0:T(8,128)(2,1)} %constant_dynamic-update-slice_fusion.32), calls=%async_computation.2 | async-start | bytes 4194304 | tf_op jit(solution)/shard_map/all_to_all | solution.py:10
  191.3 52.0 %all-to-all-done.2 = bf16[32,128,1,256]{3,1,2,0:T(8,128)(2,1)S(1)} async-done(((bf16[32,128,1,256]{3,1,2,0:T(8,128)(2,1)}), bf16[32,128,1,256]{3,1,2,0:T(8,128)(2,1)S(1)}, u32[]{:S(2)}, u32[]{:S(2)}) %all-to-all-start.2) | async-done | bytes 2097184 | tf_op jit(solution)/shard_map/all_to_all | solution.py:10
  245.4 2.4 copy.182
  247.8 6.2 %copy.188 = bf16[32,8,32,256]{3,1,2,0:T(8,128)(2,1)} copy(bf16[32,8,32,256]{3,2,1,0:T(8,128)(2,1)S(1)} %bitcast.368) | data formatting | bytes 8388608
  254.0 4.1 %convolution_convert_fusion.2 = bf16[256,128]{1,0:T(8,128)(2,1)S(1)} fusion(bf16[256,8192]{1,0:T(8,128)(2,1)} %bitcast.366, bf16[8192,128]{1,0:T(8,128)(2,1)} %all-gather.4.cloned.1.call-done), kind=kOutput, calls=%fused_computation.31 | convolution fusion | flops 536903680 | bytes 6356992 | tf_op jit(solution)/shard_map/dot_general | solution.py:108
  258.2 94.1 %all-gather.8.cloned.1.call-done = bf16[8192,1024]{1,0:T(8,128)(2,1)} async-done(((bf16[256,1024]{1,0:T(8,128)(2,1)}), bf16[8192,1024]{1,0:T(8,128)(2,1)}) %all-gather.8.cloned.1.call-update) | async-done | bytes 16777232 | tf_op jit(solution)/shard_map/all_gather | solution.py:125
  352.3 12.7 %fusion.17 = f32[256]{0:T(256)S(1)} fusion(bf16[8192,1024]{1,0:T(8,128)(2,1)} %all-gather.8.cloned.1.call-done, bf16[256,128]{1,0:T(8,128)(2,1)S(1)} %convolution_convert_fusion.2, bf16[128,8192]{1,0:T(8,128)(2,1)} %all-gather.6.cloned.1.call-done, bf16[256,8192]{1,0:T(8,128)(2,1)} %bitcast.367, f32[8192]{0:T(1024)S(1)} %copy-done.7, ...), kind=kOutput, calls=%fused_computation.30 | convolution fusion | flops 4843372544 | bytes 23176192 | tf_op jit(solution)/shard_map/dot_general | solution.py:123
  (175 shorter events, 69.9 us)
Async XLA Ops:
  7.2 180.7 %copy-start = (s32[1,4]{1,0:T(1,128)S(1)}, s32[1,4]{1,0:T(1,128)}, u32[]{:S(2)}) copy-start(s32[1,4]{1,0:T(1,128)} %param.20) | copy-start | bytes 52
  7.2 246.8 %all-gather.4.cloned.1.call-start = ((), (), s32[]{:S(2)}) async-start(), calls=%async_computation.3 | async-start | bytes 2162688 | tf_op jit(solution)/shard_map/all_gather | solution.py:110
  7.9 250.3 %all-gather.6.cloned.1.call-start = ((), (), s32[]{:S(2)}) async-start(), calls=%async_computation.4 | async-start | bytes 2162688 | tf_op jit(solution)/shard_map/all_gather | solution.py:116
  8.7 11.9 %copy-start.4 = (s32[2,4096,1,8]{1,3,2,0:T(8,128)S(1)}, s32[2,4096,1,8]{1,3,2,0:T(8,128)}, u32[]{:S(2)}) copy-start(s32[2,4096,1,8]{1,3,2,0:T(8,128)} %param.23) | copy-start | bytes 786436
  8.7 343.6 %all-gather.8.cloned.1.call-start = ((), (), s32[]{:S(2)}) async-start(), calls=%async_computation.5 | async-start | bytes 17301504 | tf_op jit(solution)/shard_map/all_gather | solution.py:125
  12.0 8.5 %copy-start.5 = (s32[2,1,4096]{2,1,0:T(1,128)S(1)}, s32[2,1,4096]{2,1,0:T(1,128)}, u32[]{:S(2)}) copy-start(s32[2,1,4096]{2,1,0:T(1,128)} %param.24) | copy-start | bytes 98308
  13.9 43.1 %all-to-all-start = ((bf16[8,1,2,128,256]{4,3,2,1,0:T(8,128)(2,1)}), bf16[8,1,2,128,256]{4,3,2,1,0:T(8,128)(2,1)S(1)}, u32[]{:S(2)}, u32[]{:S(2)}) async-start(bf16[8,1,2,128,256]{4,3,2,1,0:T(8,128)(2,1)} %broadcast_in_dim.137), calls=%async_computation | async-start | bytes 2097152 | tf_op jit(solution)/shard_map/all_to_all | solution.py:16
  52.8 2.2 copy-start.6
  52.8 4.4 %copy-start.2 = (bf16[1,4,128,256]{3,2,1,0:T(8,128)(2,1)S(1)}, bf16[1,4,128,256]{3,2,1,0:T(8,128)(2,1)}, u32[]{:S(2)}) copy-start(bf16[1,4,128,256]{3,2,1,0:T(8,128)(2,1)} %param.18) | copy-start | bytes 786436
  112.7 64.5 %all-to-all-start.1 = ((bf16[32,128,1,256]{3,1,2,0:T(8,128)(2,1)}), bf16[32,128,1,256]{3,1,2,0:T(8,128)(2,1)}, u32[]{:S(2)}, u32[]{:S(2)}) async-start(bf16[32,128,1,256]{3,1,2,0:T(8,128)(2,1)} %constant_dynamic-update-slice_fusion), calls=%async_computation.1 | async-start | bytes 4194304 | tf_op jit(solution)/shard_map/all_to_all | solution.py:10
  152.9 20.0 %copy-start.3 = (bf16[1,512,256]{2,1,0:T(8,128)(2,1)}, bf16[1,512,256]{2,1,0:T(8,128)(2,1)S(1)}, u32[]{:S(2)}) copy-start(bf16[1,512,256]{2,1,0:T(8,128)(2,1)S(1)} %get-tuple-element.320) | copy-start | bytes 786436
  172.9 17.5 %copy-start.1 = (bf16[1,8,128,256]{3,2,1,0:T(8,128)(2,1)S(1)}, bf16[1,8,128,256]{3,2,1,0:T(8,128)(2,1)}, u32[]{:S(2)}) copy-start(bf16[1,8,128,256]{3,2,1,0:T(8,128)(2,1)} %param.19) | copy-start | bytes 1572868
  177.2 66.1 %all-to-all-start.2 = ((bf16[32,128,1,256]{3,1,2,0:T(8,128)(2,1)}), bf16[32,128,1,256]{3,1,2,0:T(8,128)(2,1)S(1)}, u32[]{:S(2)}, u32[]{:S(2)}) async-start(bf16[32,128,1,256]{3,1,2,0:T(8,128)(2,1)} %constant_dynamic-update-slice_fusion.32), calls=%async_computation.2 | async-start | bytes 4194304 | tf_op jit(solution)/shard_map/all_to_all | solution.py:10
  254.0 98.3 %copy-start.7 = (f32[8192]{0:T(1024)S(1)}, f32[8192]{0:T(1024)}, u32[]{:S(2)}) copy-start(f32[8192]{0:T(1024)} %param.27) | copy-start | bytes 98308
  254.0 98.3 %copy-start.8 = (f32[1024]{0:T(1024)S(1)}, f32[1024]{0:T(1024)}, u32[]{:S(2)}) copy-start(f32[1024]{0:T(1024)} %param.30) | copy-start | bytes 12292
  254.0 98.3 %copy-start.9 = (f32[1024]{0:T(1024)S(1)}, f32[1024]{0:T(1024)}, u32[]{:S(2)}) copy-start(f32[1024]{0:T(1024)} %param.29) | copy-start | bytes 12292
Sparse Core Ops, SparseCore 0:
  10.6 76.7 all-gather.3
  89.9 95.9 all-gather.5
  188.4 163.8 all-gather.7
